TPU v7x, 32 devices: a whole 2x2x4 slice. The times are simulated.
32 devices in a mesh: member: 4 (over y, x), space: 8 (over z, core).
Axes of the slice: x: 2, y: 2, z: 4, core: 2. Of those that a mesh axis runs over, the one named last changes fastest.
Arguments:
- ensemble: float32 [128, 16, 16, 128], P(None, 'space', 'member'), may hold values from -4 to 4
- source: float32 [16, 16, 128], P('space', 'member'), may hold values from -6 to 6
- obs_rows: int32 [8, 4, 1], P('space', 'member'), may hold values from 0 to 7
- obs_values: float32 [8, 4, 128], P('space', 'member'), may hold values from -3 to 3
- obs_noise: float32 [128, 8, 4, 128], P(None, 'space', 'member'), may hold values from -5 to 5
- obs_var: float32 [8, 4, 128], P('space', 'member'), may hold values from 0.05 to 2
Outputs:
- updated: float32 [128, 16, 16, 128], P(None, 'space', 'member')
- predicted: float32 [128, 8, 4, 128], P(None, 'space', 'member')
Inputs may be any that keep to these rules, and one draw needn't show every extreme that they name: `obs_rows`: entry [s, m, o] names the cell row at (s * 2 + r // 4, m * 4 + r % 4) of the first two dimensions, whose 128 cells along the third dimension are observed; rows may repeat.
All inputs are finite; a program needn't handle non-finite values.
Results may differ from a plain program's by a relative error of at most 0.0003.
Values sent between devices are 32-bit elements; how exact they have to be, the bound alone decides.
No kernel may reach another device: no remote copies, remote signals or barrier semaphores. Data moves between devices by JAX's collectives and lax.ppermute only.
A program may use at most 64 MiB of HBM per device.

v0:
```python
import jax
import jax.numpy as jnp
from jax import lax
from jax.sharding import PartitionSpec as P

ITERS = 4


def padded_2(x, sides, width):
    for axis, dim in sides:
        devices, length = (lax.axis_size(axis), x.shape[dim])
        up = [(i, (i + 1) % devices) for i in range(devices - 1)]
        down = [(j, i) for i, j in up]
        last = lax.slice_in_dim(x, length - width, length, axis=dim)
        leading = lax.slice_in_dim(x, 0, width, axis=dim)
        before = lax.ppermute(last, axis, up)
        after = lax.ppermute(leading, axis, down)
        x = jnp.concatenate([before, x, after], axis=dim)
    return x


def harmonic(first_cond, second_cond):
    return 2.0 * first_cond * second_cond / (first_cond + second_cond)


def extend_cond(cond):
    widened = padded_2(cond, (("member", 2),), 1)
    return jnp.pad(widened, ((0, 0), (1, 1), (0, 0), (1, 1)))


def extend_values(values_in):
    widened = padded_2(values_in, (("member", 2),), 1)
    return jnp.pad(widened, ((0, 0), (1, 1), (0, 0), (1, 1)))


def member_dots(dot_terms):
    return lax.psum(dot_terms, "member")


def face_terms(cond):
    widened = extend_cond(cond)
    edge_pad = jnp.pad(cond, ((0, 0), (1, 1), (1, 1), (1, 1)), mode="edge")
    cond_pad = jnp.where(widened > 0.0, widened, edge_pad)
    face_x = harmonic(cond_pad[:, :-1, 1:-1, 1:-1], cond_pad[:, 1:, 1:-1, 1:-1])
    face_y = harmonic(cond_pad[:, 1:-1, :-1, 1:-1], cond_pad[:, 1:-1, 1:, 1:-1])
    face_z = harmonic(cond, cond_pad[:, 1:-1, 1:-1, 2:])
    lower_z = jnp.concatenate([harmonic(cond[..., :1], cond[..., :1]), face_z[..., :-1]], axis=-1)
    return (face_x, face_y, face_z, lower_z)


def operate(values_in, face_x, face_y, face_z, lower_z):
    padded = extend_values(values_in)
    result = face_x[:, 1:] * (values_in - padded[:, 2:, 1:-1, 1:-1]) + face_x[:, :-1] * (
        values_in - padded[:, :-2, 1:-1, 1:-1]
    )
    result = (
        result
        + face_y[:, :, 1:] * (values_in - padded[:, 1:-1, 2:, 1:-1])
        + face_y[:, :, :-1] * (values_in - padded[:, 1:-1, :-2, 1:-1])
    )
    result = (
        result
        + face_z * (values_in - padded[:, 1:-1, 1:-1, 2:])
        + lower_z * (values_in - padded[:, 1:-1, 1:-1, :-2])
    )
    return result


def conjugate(cond, forcing):
    face_x, face_y, face_z, lower_z = face_terms(cond)
    residual = jnp.broadcast_to(forcing[None], cond.shape)
    direction = residual
    solution = jnp.zeros_like(cond)
    norm_now = member_dots(jnp.sum(residual * residual, axis=(1, 2, 3)))
    for iteration in range(ITERS):
        image = operate(direction, face_x, face_y, face_z, lower_z)
        step_size = norm_now / member_dots(jnp.sum(direction * image, axis=(1, 2, 3)))
        solution = solution + step_size[:, None, None, None] * direction
        residual = residual - step_size[:, None, None, None] * image
        if iteration + 1 < ITERS:
            norm_next = member_dots(jnp.sum(residual * residual, axis=(1, 2, 3)))
            direction = residual + (norm_next / norm_now)[:, None, None, None] * direction
            norm_now = norm_next
    return solution


def local(ensemble, source, obs_rows, obs_values, obs_noise, obs_var):
    total_members = ensemble.shape[0]
    block_x, block_y, layers = source.shape
    held_fields = lax.all_to_all(ensemble, "space", split_axis=0, concat_axis=1, tiled=True)
    forcing = lax.all_gather(source, "space", axis=0, tiled=True)
    pressure = conjugate(jnp.exp(held_fields), forcing)
    held_count = pressure.shape[0]
    cells_flat = pressure.reshape(held_count, -1, layers)
    gathered_rows = lax.all_gather(obs_rows, "space", axis=0, tiled=True)
    row_ids = gathered_rows[:, 0]
    peer_ids = jnp.arange(row_ids.shape[0], dtype=jnp.int32)[:, None]
    flat_index = (peer_ids * block_x + row_ids // block_y) * block_y + row_ids % block_y
    picked = jnp.take(cells_flat, flat_index.reshape(-1), axis=1)
    returned = lax.all_to_all(picked, "space", split_axis=1, concat_axis=0, tiled=True)
    predicted = returned.reshape(total_members, 1, 1, -1)
    flat_pred = returned.reshape(total_members, -1)
    inv_sigma = 1.0 / jnp.sqrt(obs_var.reshape(-1))
    spread = (flat_pred - jnp.mean(flat_pred, axis=0)) * inv_sigma
    misfit = (obs_values.reshape(-1) - flat_pred) * inv_sigma + obs_noise.reshape(total_members, -1)
    gram_part = jnp.dot(spread, spread.T, precision=lax.Precision.HIGHEST)
    cross_part = jnp.dot(spread, misfit.T, precision=lax.Precision.HIGHEST)
    gram_sum, cross_sum = lax.psum((gram_part, cross_part), ("member", "space"))
    factor = jnp.linalg.cholesky(
        gram_sum + (total_members - 1.0) * jnp.eye(total_members, dtype=jnp.float32)
    )
    weights = jax.scipy.linalg.cho_solve((factor, True), cross_sum)
    flat_field = ensemble.reshape(total_members, -1)
    anomalies = flat_field - jnp.mean(flat_field, axis=0)
    updated = flat_field + jnp.dot(weights.T, anomalies, precision=lax.Precision.HIGHEST)
    return (updated.reshape(ensemble.shape), predicted)


def solution(mesh):
    in_specs = (
        P(None, "space", "member", None),
        P("space", "member", None),
        P("space", "member", None),
        P("space", "member", None),
        P(None, "space", "member", None),
        P("space", "member", None),
    )
    out_specs = (P(None, "space", "member", None), P(None, "space", "member", None))
    return jax.shard_map(local, mesh=mesh, in_specs=in_specs, out_specs=out_specs, check_vma=False)
```

profile of v0, /device:TPU:0, one launch (start us, length us, event | category | flops | bytes accessed | tf_op | source)
XLA Modules:
  0.0 352.0 jit_solution(3334532213000039188)
XLA Ops:
  7.2 6.4 %all-to-all-start = ((f32[128,2,4,128]{3,2,1,0:T(4,128)}), f32[128,2,4,128]{3,2,1,0:T(4,128)S(1)}, u32[]{:S(2)}, u32[]{:S(2)}) async-start(f32[128,2,4,128]{3,2,1,0:T(4,128)} %param.6), calls=%async_computation | async-start | bytes 1048576 | tf_op jit(solution)/shard_map/all_to_all | solution.py:90
  13.5 21.7 %all_gather.7 = f32[16,4,128]{2,1,0:T(4,128)S(1)} all-gather(f32[2,4,128]{2,1,0:T(4,128)} %param.7), channel_id=1, replica_groups=mesh['member'=4,'space'=8] {'space'}, dimensions={0}, use_global_device_ids=true | all-gather | bytes 36864 | tf_op jit(solution)/shard_map/all_gather | solution.py:91
  35.2 3.4 collective-permute-start.2
  41.9 4.8 %collective-permute-done.3 = f32[16,16,1,128]{3,0,2,1:T(8,128)S(1)} collective-permute-done((f32[16,16,1,128]{3,0,2,1:T(8,128)S(1)}, f32[16,16,1,128]{3,0,2,1:T(8,128)S(1)}, u32[]{:S(2)}, u32[]{:S(2)}) %collective-permute-start.3) | collective-permute-done | bytes 131104 | tf_op jit(solution)/shard_map/ppermute | solution.py:17
  47.3 1.7 select_maximum_fusion.6
  50.5 3.7 %collective-permute-start = (f32[16,16,1,128]{3,0,2,1:T(8,128)S(1)}, f32[16,16,1,128]{3,0,2,1:T(8,128)S(1)}, u32[]{:S(2)}, u32[]{:S(2)}) collective-permute-start(f32[16,16,1,128]{3,0,2,1:T(8,128)S(1)} %get-tuple-element.35), channel_id=1, source_target_pairs={{0,8},{8,16},{16,24},{1,9},{9,17},{17,25},{2,10},{10,18},{18,26},{... | collective-permute-start | bytes 393224 | tf_op jit(solution)/shard_map/ppermute | solution.py:16
  56.0 1.3 copy.25
  57.3 3.7 %collective-permute-done.1 = f32[16,16,1,128]{3,0,2,1:T(8,128)S(1)} collective-permute-done((f32[16,16,1,128]{3,0,2,1:T(8,128)S(1)}, f32[16,16,1,128]{3,0,2,1:T(8,128)S(1)}, u32[]{:S(2)}, u32[]{:S(2)}) %collective-permute-start.1) | collective-permute-done | bytes 131104 | tf_op jit(solution)/shard_map/ppermute | solution.py:17
  61.1 2.7 compare_select_fusion
  67.3 9.0 %all-reduce.7 = (f32[16]{0:T(128)S(1)}, f32[16]{0:T(128)S(1)}) all-reduce(f32[16]{0:T(128)S(1)} %reduce_sum.93, f32[16]{0:T(128)S(1)} %get-tuple-element.20), channel_id=1, replica_groups=mesh['member'=4,'space'=8] {'member'}, use_global_device_ids=true, to_apply=%region_1.2 | all-reduce | flops 32 | bytes 256 | tf_op jit(solution)/shard_map/psum | solution.py:37
  76.6 8.0 %psum.72 = f32[16]{0:T(128)S(1)} all-reduce(f32[16]{0:T(128)S(1)} %multiply_reduce_fusion.4), channel_id=1, replica_groups=mesh['member'=4,'space'=8] {'member'}, use_global_device_ids=true, to_apply=%region_5.6 | all-reduce | flops 16 | bytes 128 | tf_op jit(solution)/shard_map/psum | solution.py:37
  84.8 3.4 collective-permute-start.4
  90.7 4.5 %collective-permute-done.5 = f32[16,16,1,128]{3,0,2,1:T(8,128)S(1)} collective-permute-done((f32[16,16,1,128]{3,0,2,1:T(8,128)S(1)}, f32[16,16,1,128]{3,0,2,1:T(8,128)S(1)}, u32[]{:S(2)}, u32[]{:S(2)}) %collective-permute-start.5) | collective-permute-done | bytes 131104 | tf_op jit(solution)/shard_map/ppermute | solution.py:17
  95.6 1.4 multiply_reduce_fusion.3
  97.0 9.8 %psum.73 = f32[16]{0:T(128)S(1)} all-reduce(f32[16]{0:T(128)S(1)} %get-tuple-element.18), channel_id=1, replica_groups=mesh['member'=4,'space'=8] {'member'}, use_global_device_ids=true, to_apply=%region_7.8 | all-reduce | flops 16 | bytes 128 | tf_op jit(solution)/shard_map/psum | solution.py:37
  106.8 1.4 multiply_reduce_fusion.2
  108.2 8.0 %psum.74 = f32[16]{0:T(128)S(1)} all-reduce(f32[16]{0:T(128)S(1)} %get-tuple-element.16), channel_id=1, replica_groups=mesh['member'=4,'space'=8] {'member'}, use_global_device_ids=true, to_apply=%region_9.10 | all-reduce | flops 16 | bytes 128 | tf_op jit(solution)/shard_map/psum | solution.py:37
  117.0 3.5 collective-permute-start.6
  123.8 8.0 %all-reduce.5 = s32[8]{0:T(128)S(1)} all-reduce(s32[8]{0:T(128)S(1)} %bitcast_dynamic-update-slice_fusion), channel_id=1, replica_groups=mesh['member'=4,'space'=8] {'space'}, use_global_device_ids=true, to_apply=%add.5 | all-reduce | flops 8 | bytes 64 | tf_op jit(solution)/shard_map/squeeze | solution.py:96
  131.8 1.4 select_maximum_fusion.2
  133.2 2.3 multiply_reduce_fusion.1
  135.5 11.6 %psum.75 = f32[16]{0:T(128)S(1)} all-reduce(f32[16]{0:T(128)S(1)} %get-tuple-element.14), channel_id=1, replica_groups=mesh['member'=4,'space'=8] {'member'}, use_global_device_ids=true, to_apply=%region_11.12 | all-reduce | flops 16 | bytes 128 | tf_op jit(solution)/shard_map/psum | solution.py:37
  148.4 7.8 %psum.76 = f32[16]{0:T(128)S(1)} all-reduce(f32[16]{0:T(128)S(1)} %multiply_reduce_fusion), channel_id=1, replica_groups=mesh['member'=4,'space'=8] {'member'}, use_global_device_ids=true, to_apply=%region_13.14 | all-reduce | flops 16 | bytes 128 | tf_op jit(solution)/shard_map/psum | solution.py:37
  156.2 1.4 multiply_add_fusion.1
  157.6 3.7 %collective-permute-start.8 = (f32[16,16,1,128]{3,0,2,1:T(8,128)S(1)}, f32[16,16,1,128]{3,0,2,1:T(8,128)S(1)}, u32[]{:S(2)}, u32[]{:S(2)}) collective-permute-start(f32[16,16,1,128]{3,0,2,1:T(8,128)S(1)} %get-tuple-element.27), channel_id=1, source_target_pairs={{0,8},{8,16},{16,24},{1,9},{9,17},{17,25},{2,10},{10,18},{18,26},{... | collective-permute-start | bytes 393224 | tf_op jit(solution)/shard_map/ppermute | solution.py:16
  163.8 4.5 %collective-permute-done.9 = f32[16,16,1,128]{3,0,2,1:T(8,128)S(1)} collective-permute-done((f32[16,16,1,128]{3,0,2,1:T(8,128)S(1)}, f32[16,16,1,128]{3,0,2,1:T(8,128)S(1)}, u32[]{:S(2)}, u32[]{:S(2)}) %collective-permute-start.9) | collective-permute-done | bytes 131104 | tf_op jit(solution)/shard_map/ppermute | solution.py:17
  170.7 8.8 %psum.77 = f32[16]{0:T(128)S(1)} all-reduce(f32[16]{0:T(128)S(1)} %fusion.14), channel_id=1, replica_groups=mesh['member'=4,'space'=8] {'member'}, use_global_device_ids=true, to_apply=%region_15.16 | all-reduce | flops 16 | bytes 128 | tf_op jit(solution)/shard_map/psum | solution.py:37
  181.0 3.4 all-to-all-start.1
  184.7 5.6 %all-to-all-done.1 = f32[16,8,128]{2,0,1:T(8,128)S(1)} async-done(((f32[16,8,128]{2,0,1:T(8,128)}), f32[16,8,128]{2,0,1:T(8,128)S(1)}, u32[]{:S(2)}, u32[]{:S(2)}) %all-to-all-start.1) | async-done | bytes 65568 | tf_op jit(solution)/shard_map/all_to_all | solution.py:100
  192.5 124.4 %all-reduce.10.cloned.1.call-done = (f32[128,128]{1,0:T(8,128)}, f32[128,128]{1,0:T(8,128)}) async-done(((f32[128,128]{1,0:T(8,128)}, f32[128,128]{1,0:T(8,128)}), (f32[128,128]{1,0:T(8,128)}, f32[128,128]{1,0:T(8,128)})) %all-reduce.10.cloned.1.call-update) | async-done | bytes 131088 | tf_op jit(solution)/shard_map/psum | solution.py:108
  318.6 11.7 %cholesky.16 = f32[128,128]{1,0:T(8,128)S(1)} custom-call(f32[128,128]{1,0:T(8,128)S(1)} %fusion.73), custom_call_target="Cholesky" | custom-call | tf_op jit(solution)/shard_map/jit(cholesky)/cholesky | solution.py:109
  331.7 9.8 %custom-call.10 = f32[1,128,128]{1,2,0:T(8,128)S(1)} custom-call(f32[1,128,128]{2,1,0:T(8,128)S(1)} %fusion.67), custom_call_target="InvertDiagBlocksLowerTriangular" | custom-call | tf_op jit(solution)/shard_map/jit(_cho_solve)/triangular_solve | solution.py:112
  (106 shorter events, 34.4 us)
Async XLA Ops:
  7.2 41.8 %all-to-all-start = ((f32[128,2,4,128]{3,2,1,0:T(4,128)}), f32[128,2,4,128]{3,2,1,0:T(4,128)S(1)}, u32[]{:S(2)}, u32[]{:S(2)}) async-start(f32[128,2,4,128]{3,2,1,0:T(4,128)} %param.6), calls=%async_computation | async-start | bytes 1048576 | tf_op jit(solution)/shard_map/all_to_all | solution.py:90
  35.2 6.6 %collective-permute-start.2 = (f32[16,16,1,128]{3,0,2,1:T(8,128)S(1)}, f32[16,16,1,128]{3,0,2,1:T(8,128)S(1)}, u32[]{:S(2)}, u32[]{:S(2)}) collective-permute-start(f32[16,16,1,128]{3,0,2,1:T(8,128)S(1)} %broadcast_in_dim.16), channel_id=1, source_target_pairs={{0,8},{8,16},{16,24},{1,9},{9,17},{17,25},{2,10},{10,18},{18,26},{... | collective-permute-start | bytes 393224 | tf_op jit(solution)/shard_map/ppermute | solution.py:16
  38.7 8.0 %collective-permute-start.3 = (f32[16,16,1,128]{3,0,2,1:T(8,128)S(1)}, f32[16,16,1,128]{3,0,2,1:T(8,128)S(1)}, u32[]{:S(2)}, u32[]{:S(2)}) collective-permute-start(f32[16,16,1,128]{3,0,2,1:T(8,128)S(1)} %broadcast_in_dim.17), channel_id=1, source_target_pairs={{8,0},{16,8},{24,16},{9,1},{17,9},{25,17},{10,2},{18,10},{26,18},{... | collective-permute-start | bytes 393224 | tf_op jit(solution)/shard_map/ppermute | solution.py:17
  46.6 0.6 copy-start.7
  50.5 6.8 %collective-permute-start = (f32[16,16,1,128]{3,0,2,1:T(8,128)S(1)}, f32[16,16,1,128]{3,0,2,1:T(8,128)S(1)}, u32[]{:S(2)}, u32[]{:S(2)}) collective-permute-start(f32[16,16,1,128]{3,0,2,1:T(8,128)S(1)} %get-tuple-element.35), channel_id=1, source_target_pairs={{0,8},{8,16},{16,24},{1,9},{9,17},{17,25},{2,10},{10,18},{18,26},{... | collective-permute-start | bytes 393224 | tf_op jit(solution)/shard_map/ppermute | solution.py:16
  54.2 6.9 %collective-permute-start.1 = (f32[16,16,1,128]{3,0,2,1:T(8,128)S(1)}, f32[16,16,1,128]{3,0,2,1:T(8,128)S(1)}, u32[]{:S(2)}, u32[]{:S(2)}) collective-permute-start(f32[16,16,1,128]{3,0,2,1:T(8,128)S(1)} %get-tuple-element.36), channel_id=1, source_target_pairs={{8,0},{16,8},{24,16},{9,1},{17,9},{25,17},{10,2},{18,10},{26,18},{... | collective-permute-start | bytes 393224 | tf_op jit(solution)/shard_map/ppermute | solution.py:17
  64.2 1.5 copy-start
  64.2 1.6 copy-start.6
  64.2 1.6 copy-start.8
  66.7 28.9 %copy-start.2 = (f32[16,16,4,128]{3,0,2,1:T(8,128)}, f32[16,16,4,128]{3,0,2,1:T(8,128)S(1)}, u32[]{:S(2)}) copy-start(f32[16,16,4,128]{3,0,2,1:T(8,128)S(1)} %get-tuple-element.22) | copy-start | bytes 1572868
  84.8 5.9 %collective-permute-start.4 = (f32[16,16,1,128]{3,0,2,1:T(8,128)S(1)}, f32[16,16,1,128]{3,0,2,1:T(8,128)S(1)}, u32[]{:S(2)}, u32[]{:S(2)}) collective-permute-start(f32[16,16,1,128]{3,0,2,1:T(8,128)S(1)} %get-tuple-element.31), channel_id=1, source_target_pairs={{0,8},{8,16},{16,24},{1,9},{9,17},{17,25},{2,10},{10,18},{18,26},{... | collective-permute-start | bytes 393224 | tf_op jit(solution)/shard_map/ppermute | solution.py:16
  88.2 6.9 %collective-permute-start.5 = (f32[16,16,1,128]{3,0,2,1:T(8,128)S(1)}, f32[16,16,1,128]{3,0,2,1:T(8,128)S(1)}, u32[]{:S(2)}, u32[]{:S(2)}) collective-permute-start(f32[16,16,1,128]{3,0,2,1:T(8,128)S(1)} %get-tuple-element.32), channel_id=1, source_target_pairs={{8,0},{16,8},{24,16},{9,1},{17,9},{25,17},{10,2},{18,10},{26,18},{... | collective-permute-start | bytes 393224 | tf_op jit(solution)/shard_map/ppermute | solution.py:17
  106.8 15.7 %copy-start.12 = (u32[32]{0:T(128)S(1)}, u32[32]{0:T(128)}, u32[]{:S(2)}) copy-start(u32[32]{0:T(128)} %constant.131) | copy-start | bytes 388
  108.2 38.9 %copy-start.1 = (f32[16,16,4,128]{3,0,2,1:T(8,128)}, f32[16,16,4,128]{3,0,2,1:T(8,128)S(1)}, u32[]{:S(2)}) copy-start(f32[16,16,4,128]{3,0,2,1:T(8,128)S(1)} %get-tuple-element.17) | copy-start | bytes 1572868
  117.0 14.7 %collective-permute-start.6 = (f32[16,16,1,128]{3,0,2,1:T(8,128)}, f32[16,16,1,128]{3,0,2,1:T(8,128)S(1)}, u32[]{:S(2)}, u32[]{:S(2)}) collective-permute-start(f32[16,16,1,128]{3,0,2,1:T(8,128)} %get-tuple-element.29), channel_id=1, source_target_pairs={{0,8},{8,16},{16,24},{1,9},{9,17},{17,25},{2,10},{10,18},{18,26},{... | collective-permute-start | bytes 393224 | tf_op jit(solution)/shard_map/ppermute | solution.py:16
  120.6 11.2 %collective-permute-start.7 = (f32[16,16,1,128]{3,0,2,1:T(8,128)}, f32[16,16,1,128]{3,0,2,1:T(8,128)}, u32[]{:S(2)}, u32[]{:S(2)}) collective-permute-start(f32[16,16,1,128]{3,0,2,1:T(8,128)} %get-tuple-element.30), channel_id=1, source_target_pairs={{8,0},{16,8},{24,16},{9,1},{17,9},{25,17},{10,2},{18,10},{26,18},{... | collective-permute-start | bytes 393224 | tf_op jit(solution)/shard_map/ppermute | solution.py:17
  131.7 1.5 copy-start.3
  157.6 11.2 %copy-start.4 = (f32[16,16,4,128]{3,0,2,1:T(8,128)S(1)}, f32[16,16,4,128]{3,0,2,1:T(8,128)}, u32[]{:S(2)}) copy-start(f32[16,16,4,128]{3,0,2,1:T(8,128)} %copy-done.2) | copy-start | bytes 1572868
  157.6 6.2 %collective-permute-start.8 = (f32[16,16,1,128]{3,0,2,1:T(8,128)S(1)}, f32[16,16,1,128]{3,0,2,1:T(8,128)S(1)}, u32[]{:S(2)}, u32[]{:S(2)}) collective-permute-start(f32[16,16,1,128]{3,0,2,1:T(8,128)S(1)} %get-tuple-element.27), channel_id=1, source_target_pairs={{0,8},{8,16},{16,24},{1,9},{9,17},{17,25},{2,10},{10,18},{18,26},{... | collective-permute-start | bytes 393224 | tf_op jit(solution)/shard_map/ppermute | solution.py:16
  161.3 6.9 %collective-permute-start.9 = (f32[16,16,1,128]{3,0,2,1:T(8,128)S(1)}, f32[16,16,1,128]{3,0,2,1:T(8,128)S(1)}, u32[]{:S(2)}, u32[]{:S(2)}) collective-permute-start(f32[16,16,1,128]{3,0,2,1:T(8,128)S(1)} %get-tuple-element.28), channel_id=1, source_target_pairs={{8,0},{16,8},{24,16},{9,1},{17,9},{25,17},{10,2},{18,10},{26,18},{... | collective-permute-start | bytes 393224 | tf_op jit(solution)/shard_map/ppermute | solution.py:17
  169.4 15.2 %copy-start.11 = (f32[1,1,128]{2,1,0:T(1,128)S(1)}, f32[1,1,128]{2,1,0:T(1,128)}, u32[]{:S(2)}) copy-start(f32[1,1,128]{2,1,0:T(1,128)} %param.11) | copy-start | bytes 1540
  169.4 21.8 %copy-start.9 = (f32[128,1,1,128]{3,2,1,0:T(1,128)S(1)}, f32[128,1,1,128]{3,2,1,0:T(1,128)}, u32[]{:S(2)}) copy-start(f32[128,1,1,128]{3,2,1,0:T(1,128)} %param.10) | copy-start | bytes 196612
  169.4 21.8 %copy-start.10 = (f32[1,1,128]{2,1,0:T(1,128)S(1)}, f32[1,1,128]{2,1,0:T(1,128)}, u32[]{:S(2)}) copy-start(f32[1,1,128]{2,1,0:T(1,128)} %param.9) | copy-start | bytes 1540
  170.7 21.5 %copy-start.5 = (f32[128,2,4,128]{3,2,1,0:T(4,128)S(1)}, f32[128,2,4,128]{3,2,1,0:T(4,128)}, u32[]{:S(2)}) copy-start(f32[128,2,4,128]{3,2,1,0:T(4,128)} %param.6) | copy-start | bytes 1572868
  181.0 9.2 %all-to-all-start.1 = ((f32[16,8,128]{2,0,1:T(8,128)}), f32[16,8,128]{2,0,1:T(8,128)S(1)}, u32[]{:S(2)}, u32[]{:S(2)}) async-start(f32[16,8,128]{2,0,1:T(8,128)} %select_bitcast_fusion), calls=%async_computation.1 | async-start | bytes 131072 | tf_op jit(solution)/shard_map/all_to_all | solution.py:100
  184.4 132.4 %all-reduce.10.cloned.1.call-start = ((), (), s32[]{:S(2)}) async-start(), calls=%async_computation.2 | async-start | bytes 262144 | tf_op jit(solution)/shard_map/psum | solution.py:108
Sparse Core Ops, SparseCore 0:
  192.3 124.4 all-reduce.9
where the time goes:
time: 353 us; the launch traced here: 352 us
  waiting for transfers between devices  151 us (43%)
  blocking collectives  92.5 us (26%)
  other arithmetic  45.3 us (13%)
  starting transfers between devices  34.1 us (10%)
  between operations  15.2 us (4%)
  local copies, waits for them, and re-layouts  10.1 us (3%)
  matrix products  3.76 us (1%)
    psum x1, waiting for transfers between devices, local(): gram_sum, cross_sum = lax.psum((gram_part, cross_part), ('member', 'space'))  124 us
    psum x7, blocking collectives, member_dots(): return lax.psum(dot_terms, 'member')  62.8 us
    all_gather x1, blocking collectives, local(): forcing = lax.all_gather(source, 'space', axis=0, tiled=True)  21.7 us
    ppermute x5, starting transfers between devices, padded_2(): before = lax.ppermute(last, axis, up)  17.7 us
    ppermute x5, waiting for transfers between devices, padded_2(): after = lax.ppermute(leading, axis, down)  17.4 us
    another operation x3, other arithmetic, local(): jnp.linalg.cholesky(gram_sum + (total_members - 1.0) * jnp.eye(total_memb...  12.4 us
    another operation x2, other arithmetic, local(): weights = jax.scipy.linalg.cho_solve((factor, True), cross_sum)  10.5 us
    squeeze x1, blocking collectives, local(): row_ids = gathered_rows[:, 0]  7.97 us
  transfers between devices with their start and end apart: 13, of which 9 were waited for; matrix products, arithmetic and copies ran while one was open for 2% of the time, Pallas kernels for 0%

commit v1 on v0

--- a/solution.py
+++ b/solution.py
@@ -4,6 +4,12 @@
 from jax.sharding import PartitionSpec as P
 
 ITERS = 4
+
+
+def find_surface(view):
+    for pp in ("space", "member"):
+        view = jax.lax.psum(view, pp)
+    return view
 
 
 def padded_2(x, sides, width):
@@ -105,7 +111,7 @@
     misfit = (obs_values.reshape(-1) - flat_pred) * inv_sigma + obs_noise.reshape(total_members, -1)
     gram_part = jnp.dot(spread, spread.T, precision=lax.Precision.HIGHEST)
     cross_part = jnp.dot(spread, misfit.T, precision=lax.Precision.HIGHEST)
-    gram_sum, cross_sum = lax.psum((gram_part, cross_part), ("member", "space"))
+    gram_sum, cross_sum = find_surface((gram_part, cross_part))
     factor = jnp.linalg.cholesky(
         gram_sum + (total_members - 1.0) * jnp.eye(total_members, dtype=jnp.float32)
     )

time: 353 us -> 324 us (0.918)
  waiting for transfers between devices: 151 us -> 123 us
    psum x1 -> x2, waiting for transfers between devices: 124 us -> 96.3 us  [find_surface(): view = jax.lax.psum(view, pp)]
  transfers between devices with their start and end apart: 13 -> 14, of which waited for: 9 -> 10; matrix products, arithmetic and copies ran while one was open for 2% -> 2% of each run, Pallas kernels for 0% -> 0%
where the time goes in v1:
time: 324 us; the launch traced here: 323 us
  waiting for transfers between devices  123 us (38%)
  blocking collectives  92.7 us (29%)
  other arithmetic  44.2 us (14%)
  starting transfers between devices  34.1 us (11%)
  between operations  15.2 us (5%)
  local copies, waits for them, and re-layouts  10.1 us (3%)
  matrix products  3.76 us (1%)
    psum x2, waiting for transfers between devices, find_surface(): view = jax.lax.psum(view, pp)  96.3 us
    psum x7, blocking collectives, member_dots(): return lax.psum(dot_terms, 'member')  63 us
    all_gather x1, blocking collectives, local(): forcing = lax.all_gather(source, 'space', axis=0, tiled=True)  21.7 us
    ppermute x5, starting transfers between devices, padded_2(): before = lax.ppermute(last, axis, up)  17.7 us
    ppermute x5, waiting for transfers between devices, padded_2(): after = lax.ppermute(leading, axis, down)  17.3 us
    another operation x3, other arithmetic, local(): jnp.linalg.cholesky(gram_sum + (total_members - 1.0) * jnp.eye(total_memb...  12.4 us
    another operation x2, other arithmetic, local(): weights = jax.scipy.linalg.cho_solve((factor, True), cross_sum)  10.5 us
    squeeze x1, blocking collectives, local(): row_ids = gathered_rows[:, 0]  7.97 us
  transfers between devices with their start and end apart: 14, of which 10 were waited for; matrix products, arithmetic and copies ran while one was open for 2% of the time, Pallas kernels for 0%

profile of v1, /device:TPU:0, one launch (start us, length us, event | category | flops | bytes accessed | tf_op | source)
XLA Modules:
  0.0 323.2 jit_solution(3301064519038011832)
XLA Ops:
  7.2 6.4 %all-to-all-start = ((f32[128,2,4,128]{3,2,1,0:T(4,128)}), f32[128,2,4,128]{3,2,1,0:T(4,128)S(1)}, u32[]{:S(2)}, u32[]{:S(2)}) async-start(f32[128,2,4,128]{3,2,1,0:T(4,128)} %param.6), calls=%async_computation | async-start | bytes 1048576 | tf_op jit(solution)/shard_map/all_to_all | solution.py:96
  13.5 21.7 %all_gather.7 = f32[16,4,128]{2,1,0:T(4,128)S(1)} all-gather(f32[2,4,128]{2,1,0:T(4,128)} %param.7), channel_id=1, replica_groups=mesh['member'=4,'space'=8] {'space'}, dimensions={0}, use_global_device_ids=true | all-gather | bytes 36864 | tf_op jit(solution)/shard_map/all_gather | solution.py:97
  35.2 3.4 %collective-permute-start.2 = (f32[16,16,1,128]{3,0,2,1:T(8,128)S(1)}, f32[16,16,1,128]{3,0,2,1:T(8,128)S(1)}, u32[]{:S(2)}, u32[]{:S(2)}) collective-permute-start(f32[16,16,1,128]{3,0,2,1:T(8,128)S(1)} %broadcast_in_dim.16), channel_id=1, source_target_pairs={{0,8},{8,16},{16,24},{1,9},{9,17},{17,25},{2,10},{10,18},{18,26},{... | collective-permute-start | bytes 393224 | tf_op jit(solution)/shard_map/ppermute | solution.py:22
  41.9 4.8 %collective-permute-done.3 = f32[16,16,1,128]{3,0,2,1:T(8,128)S(1)} collective-permute-done((f32[16,16,1,128]{3,0,2,1:T(8,128)S(1)}, f32[16,16,1,128]{3,0,2,1:T(8,128)S(1)}, u32[]{:S(2)}, u32[]{:S(2)}) %collective-permute-start.3) | collective-permute-done | bytes 131104 | tf_op jit(solution)/shard_map/ppermute | solution.py:23
  47.3 1.7 select_maximum_fusion.6
  50.5 3.7 %collective-permute-start = (f32[16,16,1,128]{3,0,2,1:T(8,128)S(1)}, f32[16,16,1,128]{3,0,2,1:T(8,128)S(1)}, u32[]{:S(2)}, u32[]{:S(2)}) collective-permute-start(f32[16,16,1,128]{3,0,2,1:T(8,128)S(1)} %get-tuple-element.37), channel_id=1, source_target_pairs={{0,8},{8,16},{16,24},{1,9},{9,17},{17,25},{2,10},{10,18},{18,26},{... | collective-permute-start | bytes 393224 | tf_op jit(solution)/shard_map/ppermute | solution.py:22
  57.3 3.7 %collective-permute-done.1 = f32[16,16,1,128]{3,0,2,1:T(8,128)S(1)} collective-permute-done((f32[16,16,1,128]{3,0,2,1:T(8,128)S(1)}, f32[16,16,1,128]{3,0,2,1:T(8,128)S(1)}, u32[]{:S(2)}, u32[]{:S(2)}) %collective-permute-start.1) | collective-permute-done | bytes 131104 | tf_op jit(solution)/shard_map/ppermute | solution.py:23
  61.1 2.7 compare_select_fusion
  67.3 9.0 %all-reduce.7 = (f32[16]{0:T(128)S(1)}, f32[16]{0:T(128)S(1)}) all-reduce(f32[16]{0:T(128)S(1)} %reduce_sum.93, f32[16]{0:T(128)S(1)} %get-tuple-element.22), channel_id=1, replica_groups=mesh['member'=4,'space'=8] {'member'}, use_global_device_ids=true, to_apply=%region_1.2 | all-reduce | flops 32 | bytes 256 | tf_op jit(solution)/shard_map/psum | solution.py:43
  76.6 8.0 %psum.86 = f32[16]{0:T(128)S(1)} all-reduce(f32[16]{0:T(128)S(1)} %multiply_reduce_fusion.4), channel_id=1, replica_groups=mesh['member'=4,'space'=8] {'member'}, use_global_device_ids=true, to_apply=%region_5.6 | all-reduce | flops 16 | bytes 128 | tf_op jit(solution)/shard_map/psum | solution.py:43
  84.8 3.4 %collective-permute-start.4 = (f32[16,16,1,128]{3,0,2,1:T(8,128)S(1)}, f32[16,16,1,128]{3,0,2,1:T(8,128)S(1)}, u32[]{:S(2)}, u32[]{:S(2)}) collective-permute-start(f32[16,16,1,128]{3,0,2,1:T(8,128)S(1)} %get-tuple-element.33), channel_id=1, source_target_pairs={{0,8},{8,16},{16,24},{1,9},{9,17},{17,25},{2,10},{10,18},{18,26},{... | collective-permute-start | bytes 393224 | tf_op jit(solution)/shard_map/ppermute | solution.py:22
  90.7 4.5 %collective-permute-done.5 = f32[16,16,1,128]{3,0,2,1:T(8,128)S(1)} collective-permute-done((f32[16,16,1,128]{3,0,2,1:T(8,128)S(1)}, f32[16,16,1,128]{3,0,2,1:T(8,128)S(1)}, u32[]{:S(2)}, u32[]{:S(2)}) %collective-permute-start.5) | collective-permute-done | bytes 131104 | tf_op jit(solution)/shard_map/ppermute | solution.py:23
  95.6 1.4 multiply_reduce_fusion.3
  97.0 9.8 %psum.87 = f32[16]{0:T(128)S(1)} all-reduce(f32[16]{0:T(128)S(1)} %get-tuple-element.20), channel_id=1, replica_groups=mesh['member'=4,'space'=8] {'member'}, use_global_device_ids=true, to_apply=%region_7.8 | all-reduce | flops 16 | bytes 128 | tf_op jit(solution)/shard_map/psum | solution.py:43
  106.8 1.4 multiply_reduce_fusion.2
  108.2 8.0 %psum.88 = f32[16]{0:T(128)S(1)} all-reduce(f32[16]{0:T(128)S(1)} %get-tuple-element.18), channel_id=1, replica_groups=mesh['member'=4,'space'=8] {'member'}, use_global_device_ids=true, to_apply=%region_9.10 | all-reduce | flops 16 | bytes 128 | tf_op jit(solution)/shard_map/psum | solution.py:43
  117.0 3.5 %collective-permute-start.6 = (f32[16,16,1,128]{3,0,2,1:T(8,128)}, f32[16,16,1,128]{3,0,2,1:T(8,128)S(1)}, u32[]{:S(2)}, u32[]{:S(2)}) collective-permute-start(f32[16,16,1,128]{3,0,2,1:T(8,128)} %get-tuple-element.31), channel_id=1, source_target_pairs={{0,8},{8,16},{16,24},{1,9},{9,17},{17,25},{2,10},{10,18},{18,26},{... | collective-permute-start | bytes 393224 | tf_op jit(solution)/shard_map/ppermute | solution.py:22
  123.8 8.0 %all-reduce.5 = s32[8]{0:T(128)S(1)} all-reduce(s32[8]{0:T(128)S(1)} %bitcast_dynamic-update-slice_fusion), channel_id=1, replica_groups=mesh['member'=4,'space'=8] {'space'}, use_global_device_ids=true, to_apply=%add.5 | all-reduce | flops 8 | bytes 64 | tf_op jit(solution)/shard_map/squeeze | solution.py:102
  131.8 1.4 select_maximum_fusion.2
  133.2 2.3 multiply_reduce_fusion.1
  135.5 11.6 %psum.89 = f32[16]{0:T(128)S(1)} all-reduce(f32[16]{0:T(128)S(1)} %get-tuple-element.16), channel_id=1, replica_groups=mesh['member'=4,'space'=8] {'member'}, use_global_device_ids=true, to_apply=%region_11.12 | all-reduce | flops 16 | bytes 128 | tf_op jit(solution)/shard_map/psum | solution.py:43
  148.4 7.8 %psum.90 = f32[16]{0:T(128)S(1)} all-reduce(f32[16]{0:T(128)S(1)} %multiply_reduce_fusion), channel_id=1, replica_groups=mesh['member'=4,'space'=8] {'member'}, use_global_device_ids=true, to_apply=%region_13.14 | all-reduce | flops 16 | bytes 128 | tf_op jit(solution)/shard_map/psum | solution.py:43
  156.2 1.4 multiply_add_fusion.1
  157.6 3.7 %collective-permute-start.8 = (f32[16,16,1,128]{3,0,2,1:T(8,128)S(1)}, f32[16,16,1,128]{3,0,2,1:T(8,128)S(1)}, u32[]{:S(2)}, u32[]{:S(2)}) collective-permute-start(f32[16,16,1,128]{3,0,2,1:T(8,128)S(1)} %get-tuple-element.29), channel_id=1, source_target_pairs={{0,8},{8,16},{16,24},{1,9},{9,17},{17,25},{2,10},{10,18},{18,26},{... | collective-permute-start | bytes 393224 | tf_op jit(solution)/shard_map/ppermute | solution.py:22
  163.8 4.4 %collective-permute-done.9 = f32[16,16,1,128]{3,0,2,1:T(8,128)S(1)} collective-permute-done((f32[16,16,1,128]{3,0,2,1:T(8,128)S(1)}, f32[16,16,1,128]{3,0,2,1:T(8,128)S(1)}, u32[]{:S(2)}, u32[]{:S(2)}) %collective-permute-start.9) | collective-permute-done | bytes 131104 | tf_op jit(solution)/shard_map/ppermute | solution.py:23
  169.4 9.0 %psum.91 = f32[16]{0:T(128)S(1)} all-reduce(f32[16]{0:T(128)S(1)} %fusion.14), channel_id=1, replica_groups=mesh['member'=4,'space'=8] {'member'}, use_global_device_ids=true, to_apply=%region_15.16 | all-reduce | flops 16 | bytes 128 | tf_op jit(solution)/shard_map/psum | solution.py:43
  179.9 3.4 %all-to-all-start.1 = ((f32[16,8,128]{2,0,1:T(8,128)}), f32[16,8,128]{2,0,1:T(8,128)S(1)}, u32[]{:S(2)}, u32[]{:S(2)}) async-start(f32[16,8,128]{2,0,1:T(8,128)} %select_bitcast_fusion), calls=%async_computation.1 | async-start | bytes 131072 | tf_op jit(solution)/shard_map/all_to_all | solution.py:106
  183.4 5.8 %all-to-all-done.1 = f32[16,8,128]{2,0,1:T(8,128)S(1)} async-done(((f32[16,8,128]{2,0,1:T(8,128)}), f32[16,8,128]{2,0,1:T(8,128)S(1)}, u32[]{:S(2)}, u32[]{:S(2)}) %all-to-all-start.1) | async-done | bytes 65568 | tf_op jit(solution)/shard_map/all_to_all | solution.py:106
  191.7 52.1 %all-reduce.12.cloned.1.call-done = (f32[128,128]{1,0:T(8,128)}, f32[128,128]{1,0:T(8,128)}) async-done(((f32[128,128]{1,0:T(8,128)}, f32[128,128]{1,0:T(8,128)}), (f32[128,128]{1,0:T(8,128)}, f32[128,128]{1,0:T(8,128)})) %all-reduce.12.cloned.1.call-update) | async-done | bytes 131088 | tf_op jit(solution)/shard_map/psum | solution.py:11
  243.9 44.2 %all-reduce.14.cloned.1.call-done = (f32[128,128]{1,0:T(8,128)}, f32[128,128]{1,0:T(8,128)}) async-done(((f32[128,128]{1,0:T(8,128)}, f32[128,128]{1,0:T(8,128)}), (f32[128,128]{1,0:T(8,128)}, f32[128,128]{1,0:T(8,128)})) %all-reduce.14.cloned.1.call-update) | async-done | bytes 131088 | tf_op jit(solution)/shard_map/psum | solution.py:11
  289.9 11.7 %cholesky.16 = f32[128,128]{1,0:T(8,128)S(1)} custom-call(f32[128,128]{1,0:T(8,128)S(1)} %fusion.73), custom_call_target="Cholesky" | custom-call | tf_op jit(solution)/shard_map/jit(cholesky)/cholesky | solution.py:115
  302.9 9.8 %custom-call.10 = f32[1,128,128]{1,2,0:T(8,128)S(1)} custom-call(f32[1,128,128]{2,1,0:T(8,128)S(1)} %fusion.67), custom_call_target="InvertDiagBlocksLowerTriangular" | custom-call | tf_op jit(solution)/shard_map/jit(_cho_solve)/triangular_solve | solution.py:118
  (109 shorter events, 34.8 us)
Async XLA Ops:
  7.2 41.8 %all-to-all-start = ((f32[128,2,4,128]{3,2,1,0:T(4,128)}), f32[128,2,4,128]{3,2,1,0:T(4,128)S(1)}, u32[]{:S(2)}, u32[]{:S(2)}) async-start(f32[128,2,4,128]{3,2,1,0:T(4,128)} %param.6), calls=%async_computation | async-start | bytes 1048576 | tf_op jit(solution)/shard_map/all_to_all | solution.py:96
  35.2 6.6 %collective-permute-start.2 = (f32[16,16,1,128]{3,0,2,1:T(8,128)S(1)}, f32[16,16,1,128]{3,0,2,1:T(8,128)S(1)}, u32[]{:S(2)}, u32[]{:S(2)}) collective-permute-start(f32[16,16,1,128]{3,0,2,1:T(8,128)S(1)} %broadcast_in_dim.16), channel_id=1, source_target_pairs={{0,8},{8,16},{16,24},{1,9},{9,17},{17,25},{2,10},{10,18},{18,26},{... | collective-permute-start | bytes 393224 | tf_op jit(solution)/shard_map/ppermute | solution.py:22
  38.7 8.0 %collective-permute-start.3 = (f32[16,16,1,128]{3,0,2,1:T(8,128)S(1)}, f32[16,16,1,128]{3,0,2,1:T(8,128)S(1)}, u32[]{:S(2)}, u32[]{:S(2)}) collective-permute-start(f32[16,16,1,128]{3,0,2,1:T(8,128)S(1)} %broadcast_in_dim.17), channel_id=1, source_target_pairs={{8,0},{16,8},{24,16},{9,1},{17,9},{25,17},{10,2},{18,10},{26,18},{... | collective-permute-start | bytes 393224 | tf_op jit(solution)/shard_map/ppermute | solution.py:23
  46.6 0.6 copy-start.7
  50.5 6.8 %collective-permute-start = (f32[16,16,1,128]{3,0,2,1:T(8,128)S(1)}, f32[16,16,1,128]{3,0,2,1:T(8,128)S(1)}, u32[]{:S(2)}, u32[]{:S(2)}) collective-permute-start(f32[16,16,1,128]{3,0,2,1:T(8,128)S(1)} %get-tuple-element.37), channel_id=1, source_target_pairs={{0,8},{8,16},{16,24},{1,9},{9,17},{17,25},{2,10},{10,18},{18,26},{... | collective-permute-start | bytes 393224 | tf_op jit(solution)/shard_map/ppermute | solution.py:22
  54.2 6.9 %collective-permute-start.1 = (f32[16,16,1,128]{3,0,2,1:T(8,128)S(1)}, f32[16,16,1,128]{3,0,2,1:T(8,128)S(1)}, u32[]{:S(2)}, u32[]{:S(2)}) collective-permute-start(f32[16,16,1,128]{3,0,2,1:T(8,128)S(1)} %get-tuple-element.38), channel_id=1, source_target_pairs={{8,0},{16,8},{24,16},{9,1},{17,9},{25,17},{10,2},{18,10},{26,18},{... | collective-permute-start | bytes 393224 | tf_op jit(solution)/shard_map/ppermute | solution.py:23
  64.2 1.5 copy-start
  64.2 1.6 copy-start.6
  64.2 1.6 copy-start.8
  66.7 28.9 %copy-start.2 = (f32[16,16,4,128]{3,0,2,1:T(8,128)}, f32[16,16,4,128]{3,0,2,1:T(8,128)S(1)}, u32[]{:S(2)}) copy-start(f32[16,16,4,128]{3,0,2,1:T(8,128)S(1)} %get-tuple-element.24) | copy-start | bytes 1572868
  84.8 5.9 %collective-permute-start.4 = (f32[16,16,1,128]{3,0,2,1:T(8,128)S(1)}, f32[16,16,1,128]{3,0,2,1:T(8,128)S(1)}, u32[]{:S(2)}, u32[]{:S(2)}) collective-permute-start(f32[16,16,1,128]{3,0,2,1:T(8,128)S(1)} %get-tuple-element.33), channel_id=1, source_target_pairs={{0,8},{8,16},{16,24},{1,9},{9,17},{17,25},{2,10},{10,18},{18,26},{... | collective-permute-start | bytes 393224 | tf_op jit(solution)/shard_map/ppermute | solution.py:22
  88.2 6.9 %collective-permute-start.5 = (f32[16,16,1,128]{3,0,2,1:T(8,128)S(1)}, f32[16,16,1,128]{3,0,2,1:T(8,128)S(1)}, u32[]{:S(2)}, u32[]{:S(2)}) collective-permute-start(f32[16,16,1,128]{3,0,2,1:T(8,128)S(1)} %get-tuple-element.34), channel_id=1, source_target_pairs={{8,0},{16,8},{24,16},{9,1},{17,9},{25,17},{10,2},{18,10},{26,18},{... | collective-permute-start | bytes 393224 | tf_op jit(solution)/shard_map/ppermute | solution.py:23
  106.8 15.7 %copy-start.12 = (u32[32]{0:T(128)S(1)}, u32[32]{0:T(128)}, u32[]{:S(2)}) copy-start(u32[32]{0:T(128)} %constant.131) | copy-start | bytes 388
  108.2 38.9 %copy-start.1 = (f32[16,16,4,128]{3,0,2,1:T(8,128)}, f32[16,16,4,128]{3,0,2,1:T(8,128)S(1)}, u32[]{:S(2)}) copy-start(f32[16,16,4,128]{3,0,2,1:T(8,128)S(1)} %get-tuple-element.19) | copy-start | bytes 1572868
  117.0 14.7 %collective-permute-start.6 = (f32[16,16,1,128]{3,0,2,1:T(8,128)}, f32[16,16,1,128]{3,0,2,1:T(8,128)S(1)}, u32[]{:S(2)}, u32[]{:S(2)}) collective-permute-start(f32[16,16,1,128]{3,0,2,1:T(8,128)} %get-tuple-element.31), channel_id=1, source_target_pairs={{0,8},{8,16},{16,24},{1,9},{9,17},{17,25},{2,10},{10,18},{18,26},{... | collective-permute-start | bytes 393224 | tf_op jit(solution)/shard_map/ppermute | solution.py:22
  120.6 11.2 %collective-permute-start.7 = (f32[16,16,1,128]{3,0,2,1:T(8,128)}, f32[16,16,1,128]{3,0,2,1:T(8,128)}, u32[]{:S(2)}, u32[]{:S(2)}) collective-permute-start(f32[16,16,1,128]{3,0,2,1:T(8,128)} %get-tuple-element.32), channel_id=1, source_target_pairs={{8,0},{16,8},{24,16},{9,1},{17,9},{25,17},{10,2},{18,10},{26,18},{... | collective-permute-start | bytes 393224 | tf_op jit(solution)/shard_map/ppermute | solution.py:23
  131.7 1.5 copy-start.3
  157.6 11.1 %copy-start.4 = (f32[16,16,4,128]{3,0,2,1:T(8,128)S(1)}, f32[16,16,4,128]{3,0,2,1:T(8,128)}, u32[]{:S(2)}) copy-start(f32[16,16,4,128]{3,0,2,1:T(8,128)} %copy-done.2) | copy-start | bytes 1572868
  157.6 6.2 %collective-permute-start.8 = (f32[16,16,1,128]{3,0,2,1:T(8,128)S(1)}, f32[16,16,1,128]{3,0,2,1:T(8,128)S(1)}, u32[]{:S(2)}, u32[]{:S(2)}) collective-permute-start(f32[16,16,1,128]{3,0,2,1:T(8,128)S(1)} %get-tuple-element.29), channel_id=1, source_target_pairs={{0,8},{8,16},{16,24},{1,9},{9,17},{17,25},{2,10},{10,18},{18,26},{... | collective-permute-start | bytes 393224 | tf_op jit(solution)/shard_map/ppermute | solution.py:22
  161.3 6.9 %collective-permute-start.9 = (f32[16,16,1,128]{3,0,2,1:T(8,128)S(1)}, f32[16,16,1,128]{3,0,2,1:T(8,128)S(1)}, u32[]{:S(2)}, u32[]{:S(2)}) collective-permute-start(f32[16,16,1,128]{3,0,2,1:T(8,128)S(1)} %get-tuple-element.30), channel_id=1, source_target_pairs={{8,0},{16,8},{24,16},{9,1},{17,9},{25,17},{10,2},{18,10},{26,18},{... | collective-permute-start | bytes 393224 | tf_op jit(solution)/shard_map/ppermute | solution.py:23
  169.3 14.0 %copy-start.11 = (f32[1,1,128]{2,1,0:T(1,128)S(1)}, f32[1,1,128]{2,1,0:T(1,128)}, u32[]{:S(2)}) copy-start(f32[1,1,128]{2,1,0:T(1,128)} %param.11) | copy-start | bytes 1540
  169.3 20.7 %copy-start.9 = (f32[128,1,1,128]{3,2,1,0:T(1,128)S(1)}, f32[128,1,1,128]{3,2,1,0:T(1,128)}, u32[]{:S(2)}) copy-start(f32[128,1,1,128]{3,2,1,0:T(1,128)} %param.10) | copy-start | bytes 196612
  169.4 20.7 %copy-start.10 = (f32[1,1,128]{2,1,0:T(1,128)S(1)}, f32[1,1,128]{2,1,0:T(1,128)}, u32[]{:S(2)}) copy-start(f32[1,1,128]{2,1,0:T(1,128)} %param.9) | copy-start | bytes 1540
  169.4 22.0 %copy-start.5 = (f32[128,2,4,128]{3,2,1,0:T(4,128)S(1)}, f32[128,2,4,128]{3,2,1,0:T(4,128)}, u32[]{:S(2)}) copy-start(f32[128,2,4,128]{3,2,1,0:T(4,128)} %param.6) | copy-start | bytes 1572868
  179.9 9.2 %all-to-all-start.1 = ((f32[16,8,128]{2,0,1:T(8,128)}), f32[16,8,128]{2,0,1:T(8,128)S(1)}, u32[]{:S(2)}, u32[]{:S(2)}) async-start(f32[16,8,128]{2,0,1:T(8,128)} %select_bitcast_fusion), calls=%async_computation.1 | async-start | bytes 131072 | tf_op jit(solution)/shard_map/all_to_all | solution.py:106
  183.3 60.5 %all-reduce.12.cloned.1.call-start = ((), (), s32[]{:S(2)}) async-start(), calls=%async_computation.2 | async-start | bytes 262144 | tf_op jit(solution)/shard_map/psum | solution.py:11
  191.1 96.9 %all-reduce.14.cloned.1.call-start = ((), (), s32[]{:S(2)}) async-start(), calls=%async_computation.3 | async-start | bytes 262144 | tf_op jit(solution)/shard_map/psum | solution.py:11
Sparse Core Ops, SparseCore 0:
  191.2 52.5 all-reduce.11
  246.7 41.3 all-reduce.13
